TPU v7x, 32 devices: a whole 2x2x4 slice. The times are simulated.
32 devices in a mesh: grp: 8 (over z, y), tp: 4 (over x, core).
Axes of the slice: x: 2, y: 2, z: 4, core: 2. Of those that a mesh axis runs over, the one named last changes fastest.
Arguments:
- source_rows: bfloat16 [4096, 2048], P('grp', 'tp'), may hold values from -0.09375 to 0.09375
- span_order: int32 [8], replicated, may hold values from 0 to 7, each once
- head_map: int32 [8], replicated, may hold values from 0 to 7, as said below
Outputs:
- packed: float32 [2048, 4096], P('tp')
Inputs may be any that keep to these rules, and one draw needn't show every extreme that they name: `span_order`: a permutation of the 8 row blocks. `head_map`: a permutation of the 8 heads in which slot i of serving shard s takes a head of trainer shard (s + 2 + i) mod 4, trainer shard k holding heads k * 2 to k * 2 + 1.
All inputs are finite; a program needn't handle non-finite values.
Results may differ from a plain program's by a relative error of at most 0.0003.
Values may be sent and summed in bfloat16 or wider, within the bound.
A program may use at most 64 MiB of HBM per device.

v0:
```python
import jax
import jax.numpy as jnp
from jax import lax
from jax.sharding import PartitionSpec as P


def invert_order(span_order):
    block_count = span_order.shape[0]
    positions = jnp.arange(block_count, dtype=jnp.int32)
    matches = (span_order[:, None] == positions[None, :]).astype(jnp.int32)
    return jnp.sum(matches * positions[:, None], axis=0)


def reorder_rows(gathered, inverse, row_count):
    block_count = inverse.shape[0]
    blocks = gathered.reshape(block_count, row_count, gathered.shape[1])
    return jnp.take(blocks, inverse, axis=0).reshape(block_count * row_count, gathered.shape[1])


def local(source_rows, span_order, head_map):
    row_count = source_rows.shape[0]
    shard_heads = head_map.shape[0] // lax.axis_size("tp")
    head_size = source_rows.shape[1] // (2 * shard_heads)
    all_heads = head_map.shape[0]
    wanted = lax.dynamic_slice_in_dim(head_map, lax.axis_index("tp") * shard_heads, shard_heads)
    inverse = invert_order(span_order)
    gathered = lax.all_gather(source_rows, "tp", axis=1, tiled=True)
    heads = gathered.reshape(row_count, all_heads, 2, head_size)
    picked = jnp.take(heads, wanted, axis=1)
    picked = picked.transpose(0, 2, 1, 3).reshape(row_count, 2 * shard_heads * head_size)
    every_row = lax.all_gather(picked, "grp", axis=0, tiled=True)
    ordered = reorder_rows(every_row, inverse, row_count)
    packed = ordered.T.astype(jnp.float32)
    return packed


def solution(mesh):
    placed = (P("grp", "tp"), P(), P())
    return jax.shard_map(
        local, mesh=mesh, in_specs=placed, out_specs=P("tp", None), check_vma=False
    )
```

profile of v0, /device:TPU:0, one launch (start us, length us, event | category | flops | bytes accessed | tf_op | source)
XLA Modules:
  0.0 144.5 jit_solution(5900472316146953299)
XLA Ops:
  6.5 0.0 all-gather.3.cloned.1.call-start
  6.5 2.0 %copy.14 = bf16[512,512]{0,1:T(8,128)(2,1)} copy(bf16[512,512]{1,0:T(8,128)(2,1)} %param.3) | data formatting | bytes 1048576 | tf_op args[0]
  8.6 0.0 copy-start
  8.6 0.0 all-gather.3.cloned.1.call-update
  8.6 0.0 all-gather.5.cloned.1.call-start
  8.7 0.7 compare_and_fusion
  9.4 24.8 %all-gather.3.cloned.1.call-done = bf16[512,2048]{0,1:T(8,128)(2,1)} async-done(((bf16[512,512]{0,1:T(8,128)(2,1)}), bf16[512,2048]{0,1:T(8,128)(2,1)}) %all-gather.3.cloned.1.call-update) | async-done | bytes 2097168 | tf_op jit(solution)/shard_map/all_gather | solution.py:27
  34.2 3.0 %copy.15 = bf16[512,8,2,128]{3,0,2,1:T(8,128)(2,1)S(1)} copy(bf16[512,8,2,128]{0,3,2,1:T(8,128)(2,1)} %bitcast.17) | data formatting | bytes 4194304 | tf_op jit(solution)/shard_map/reshape | solution.py:28
  37.2 0.6 gather_fusion
  37.9 0.1 select_bitcast_fusion
  38.0 1.0 copy.16
  39.0 0.0 all-gather.5.cloned.1.call-update
  39.1 0.0 copy-done
  39.1 0.1 select_reduce_fusion
  39.2 0.1 broadcast_bitcast_fusion
  39.3 74.6 %all-gather.5.cloned.1.call-done = bf16[4096,512]{0,1:T(8,128)(2,1)} async-done(((bf16[512,512]{0,1:T(8,128)(2,1)}), bf16[4096,512]{0,1:T(8,128)(2,1)}) %all-gather.5.cloned.1.call-update) | async-done | bytes 4194320 | tf_op jit(solution)/shard_map/all_gather | solution.py:31
  113.8 6.4 %copy.17 = bf16[4096,512]{1,0:T(8,128)(2,1)} copy(bf16[4096,512]{0,1:T(8,128)(2,1)} %all-gather.5.cloned.1.call-done) | data formatting | bytes 8388608 | tf_op jit(solution)/shard_map/all_gather | solution.py:31
  120.2 4.9 %gather_fusion.1 = bf16[8,512,512]{2,1,0:T(8,128)(2,1)} fusion(bf16[8,512,512]{2,1,0:T(8,128)(2,1)} %bitcast.15, s32[1024]{0:T(1024)S(1)} %pad_clamp_fusion), kind=kCustom, calls=%fused_computation.1 | custom fusion | bytes 8388640 | tf_op jit(solution)/shard_map/jit(_take)/gather | solution.py:17
  125.2 6.4 %copy.18 = bf16[4096,512]{0,1:T(8,128)(2,1)} copy(bf16[4096,512]{1,0:T(8,128)(2,1)} %bitcast.16) | data formatting | bytes 8388608 | tf_op jit(solution)/shard_map/jit(_take)/gather | solution.py:17
  131.5 6.1 %convert_bitcast_fusion = f32[512,4096]{1,0:T(8,128)} fusion(bf16[4096,512]{0,1:T(8,128)(2,1)} %copy.18, pred[4096]{0:T(1024)(128)(4,1)S(1)} %bitcast.19), kind=kLoop, calls=%fused_computation.2 | loop fusion | flops 4194304 | bytes 12587008 | tf_op jit(solution)/shard_map/convert_element_type | solution.py:33
  (5 shorter events, 0.0 us)
Async XLA Ops:
  6.5 27.7 %all-gather.3.cloned.1.call-start = ((), (), s32[]{:S(2)}) async-start(), calls=%async_computation | async-start | bytes 2621440 | tf_op jit(solution)/shard_map/all_gather | solution.py:27
  8.6 30.5 %copy-start = (s32[8]{0:T(128)S(1)}, s32[8]{0:T(128)}, u32[]{:S(2)}) copy-start(s32[8]{0:T(128)} %param.4) | copy-start | bytes 100
  8.6 105.2 %all-gather.5.cloned.1.call-start = ((), (), s32[]{:S(2)}) async-start(), calls=%async_computation.1 | async-start | bytes 4718592 | tf_op jit(solution)/shard_map/all_gather | solution.py:31
Sparse Core Ops, SparseCore 0:
  8.9 25.2 all-gather.2
  39.2 74.6 all-gather.4
where the time goes:
time: 145 us
  waiting for transfers between devices  99.4 us (69%)
  local copies, waits for them, and re-layouts  24.5 us (17%)
  between operations  13.5 us (9%)
  other arithmetic  7.1 us (5%)
    all_gather x1, waiting for transfers between devices, local(): every_row = lax.all_gather(picked, 'grp', axis=0, tiled=True)  74.6 us
    all_gather x1, waiting for transfers between devices, local(): gathered = lax.all_gather(source_rows, 'tp', axis=1, tiled=True)  24.8 us
    gather x2, local copies, waits for them, and re-layouts, reorder_rows(): jnp.take(blocks, inverse, axis=0)  11.3 us
    all_gather x1, local copies, waits for them, and re-layouts, local(): every_row = lax.all_gather(picked, 'grp', axis=0, tiled=True)  6.4 us
    convert_element_type x1, other arithmetic, local(): packed = ordered.T.astype(jnp.float32)  6.14 us
    reshape x1, local copies, waits for them, and re-layouts, local(): heads = gathered.reshape(row_count, all_heads, 2, head_size)  3.03 us
  transfers between devices with their start and end apart: 2, of which 2 were waited for; matrix products, arithmetic and copies ran while one was open for 1% of the time, Pallas kernels for 0%

commit v1 on v0

v1 whole, which is shorter than its diff:
```python
import functools

import jax
import jax.numpy as jnp
from jax import lax
from jax.experimental import pallas as pl
from jax.experimental.pallas import tpu as pltpu
from jax.sharding import PartitionSpec as P

MESH = pl.DeviceIdType.MESH
CHUNKS = 2


def ring_member(position, n):
    half = position // (n // 2)
    return 2 * position * (1 - half) + (2 * (n - 1 - position) + 1) * half


def ring_position(member, n):
    odd = member % 2
    return (member // 2) * (1 - odd) + (n - 1 - member // 2) * odd


def gather_kernel(n, tp, pieces, gathered, x_send, x_recv, r_send, r_recv):
    slots, rows = pieces.shape[0], pieces.shape[1]
    me, k = lax.axis_index("grp"), lax.axis_index("tp")
    position = ring_position(me, n)
    ring = [ring_member((position + 1) % n, n), ring_member((position + n - 1) % n, n)]
    size = rows // (2 * CHUNKS)
    parts = [(c, i) for c in range(CHUNKS) for i in reversed(range(slots))]

    barrier = pltpu.get_barrier_semaphore()
    for step in range(1, tp):
        pl.semaphore_signal(barrier, inc=1, device_id=(me, (k + step) % tp), device_id_type=MESH)
    for other in ring:
        pl.semaphore_signal(barrier, inc=1, device_id=(other, k), device_id_type=MESH)
    pl.semaphore_wait(barrier, tp + 1)

    def exchange(at, way):
        c, i = parts[at]
        span = pl.ds((way * CHUNKS + c) * size, size)
        return pltpu.make_async_remote_copy(
            src_ref=pieces.at[i, span],
            dst_ref=gathered.at[me, i, span],
            send_sem=x_send.at[way, at],
            recv_sem=x_recv.at[way, at],
            device_id=(me, (k + 2 * tp - tp // 2 - i) % tp),
            device_id_type=MESH,
        )

    def hop(step, at, way):
        c, i = parts[at]
        span = pl.ds((way * CHUNKS + c) * size, size)
        owner = ring_member((position + (n - step if way == 0 else step)) % n, n)
        return pltpu.make_async_remote_copy(
            src_ref=gathered.at[owner, i, span],
            dst_ref=gathered.at[owner, i, span],
            send_sem=r_send.at[step, way, at],
            recv_sem=r_recv.at[step, way, at],
            device_id=(ring[way], k),
            device_id_type=MESH,
        )

    for at in range(len(parts)):
        for way in range(2):
            exchange(at, way).start()
    for at in range(len(parts)):
        for way in range(2):
            exchange(at, way).wait_recv()
            hop(0, at, way).start()

    def forward(step, carry):
        for at in range(len(parts)):
            for way in range(2):
                hop(step - 1, at, way).wait_recv()
                hop(step, at, way).start()
        return carry

    lax.fori_loop(1, n - 1, forward, 0)
    for at in range(len(parts)):
        for way in range(2):
            hop(n - 2, at, way).wait_recv()
            exchange(at, way).wait_send()

    def drain(step, carry):
        for at in range(len(parts)):
            for way in range(2):
                hop(step, at, way).wait_send()
        return carry

    lax.fori_loop(0, n - 1, drain, 0)


def pack_kernel(inverse, *refs):
    blocks, out = refs[:-1], refs[-1]
    slots, width = blocks[0].shape[1], blocks[0].shape[3] // 2
    for c in range(2):
        for i in range(slots):
            cut = [b[0, i, :, c * width:(c + 1) * width].astype(jnp.float32) for b in blocks]
            whole = cut[0] if len(cut) == 1 else jnp.concatenate(cut, axis=0)
            out[pl.ds((c * slots + i) * width, width), :] = whole.T


def invert_order(span_order):
    block_count = span_order.shape[0]
    positions = jnp.arange(block_count, dtype=jnp.int32)
    matches = (span_order[:, None] == positions[None, :]).astype(jnp.int32)
    return jnp.sum(matches * positions[:, None], axis=0)


def local(n, tp, source_rows, span_order, head_map):
    rows = source_rows.shape[0]
    slots = head_map.shape[0] // tp
    columns = source_rows.shape[1] // slots
    k = lax.axis_index("tp")
    heads = source_rows.reshape(rows, slots, columns)
    pieces = []
    for i in range(slots):
        served = lax.rem(k + 2 * tp - tp // 2 - i, tp)
        head = lax.dynamic_index_in_dim(head_map, served * slots + i, keepdims=False) - k * slots
        pieces.append(lax.dynamic_index_in_dim(heads, head, axis=1, keepdims=False))
    pieces = jnp.stack(pieces)
    parts = CHUNKS * slots
    gathered = pl.pallas_call(
        functools.partial(gather_kernel, n, tp),
        out_shape=jax.ShapeDtypeStruct((n, slots, rows, columns), source_rows.dtype),
        in_specs=[pl.BlockSpec(memory_space=pl.ANY)],
        out_specs=pl.BlockSpec(memory_space=pl.ANY),
        scratch_shapes=[
            pltpu.SemaphoreType.DMA((2, parts)),
            pltpu.SemaphoreType.DMA((2, parts)),
            pltpu.SemaphoreType.DMA((n - 1, 2, parts)),
            pltpu.SemaphoreType.DMA((n - 1, 2, parts)),
        ],
        compiler_params=pltpu.CompilerParams(
            collective_id=0, has_side_effects=True, vmem_limit_bytes=8 * 1024 * 1024
        ),
        name="gather",
    )(pieces)
    inverse = invert_order(span_order)
    together = max(1, 128 // rows)
    packed = pl.pallas_call(
        pack_kernel,
        out_shape=jax.ShapeDtypeStruct((slots * columns, n * rows), jnp.float32),
        grid_spec=pltpu.PrefetchScalarGridSpec(
            num_scalar_prefetch=1,
            grid=(n // together,),
            in_specs=[
                pl.BlockSpec(
                    (1, slots, rows, columns),
                    functools.partial(lambda j, b, inv: (inv[b * together + j], 0, 0, 0), j),
                )
                for j in range(together)
            ],
            out_specs=pl.BlockSpec((slots * columns, together * rows), lambda b, inv: (0, b)),
        ),
        compiler_params=pltpu.CompilerParams(vmem_limit_bytes=16 * 1024 * 1024),
        name="pack",
    )(inverse, *[gathered] * together)
    return packed


def solution(mesh):
    n, tp = mesh.shape["grp"], mesh.shape["tp"]
    placed = (P("grp", "tp"), P(), P())
    return jax.shard_map(
        functools.partial(local, n, tp), mesh=mesh, in_specs=placed,
        out_specs=P("tp", None), check_vma=False,
    )
```

time: 145 us -> 63.6 us (0.44)
  waiting for transfers between devices: 99.4 us -> 0 us
  Pallas kernels: 0 us -> 57.7 us
  local copies, waits for them, and re-layouts: 24.5 us -> 3.66 us
  between operations: 13.5 us -> 1.26 us
  other arithmetic: 7.1 us -> 0.79 us
    all_gather x2 -> x0, waiting for transfers between devices: 99.4 us -> none  [the longest x1 74.6 us: local(): every_row = lax.all_gather(picked, 'grp', axis=0, tiled=True)]
    pallas_call x0 -> x2, Pallas kernels: none -> 57.7 us  [the longest x1 52.1 us: local(): pl.pallas_call(functools.partial(gather_kernel, n, tp), out_shape=jax.Sha...]
    gather x3 -> x0, local copies, waits for them, and re-layouts: 11.9 us -> none  [the longest x2 11.3 us: reorder_rows(): jnp.take(blocks, inverse, axis=0)]
    all_gather x1 -> x0, local copies, waits for them, and re-layouts: 6.4 us -> none  [local(): every_row = lax.all_gather(picked, 'grp', axis=0, tiled=True)]
    convert_element_type x1 -> x0, other arithmetic: 6.14 us -> none  [local(): packed = ordered.T.astype(jnp.float32)]
    dynamic_slice x0 -> x2, local copies, waits for them, and re-layouts: none -> 2.4 us  [the longest x1 1.31 us: local(): lax.dynamic_index_in_dim(head_map, served * slots + i, keepdims=False)]
    unnamed x5 -> x0, local copies, waits for them, and re-layouts: 2.14 us -> none
    reshape x1, local copies, waits for them, and re-layouts: 3.03 us -> 1.16 us  [local(): heads = source_rows.reshape(rows, slots, columns)]
  transfers between devices with their start and end apart: 2 -> 0, of which waited for: 2 -> 0; matrix products, arithmetic and copies ran while one was open for 1% -> 0% of each run, Pallas kernels for 0% -> 0%
where the time goes in v1:
time: 63.6 us; the launch traced here: 63.4 us
  Pallas kernels  57.7 us (91%)
  local copies, waits for them, and re-layouts  3.66 us (6%)
  between operations  1.26 us (2%)
  other arithmetic  0.79 us (1%)
    pallas_call x1, Pallas kernels, local(): pl.pallas_call(functools.partial(gather_kernel, n, tp), out_shape=jax.Sha...  52.1 us
    pallas_call x1, Pallas kernels, local(): pl.pallas_call(pack_kernel, out_shape=jax.ShapeDtypeStruct((slots * colum...  5.61 us
    dynamic_slice x1, local copies, waits for them, and re-layouts, local(): lax.dynamic_index_in_dim(head_map, served * slots + i, keepdims=False)  1.31 us

profile of v1, /device:TPU:0, one launch (start us, length us, event | category | flops | bytes accessed | tf_op | source)
XLA Modules:
  0.0 63.4 jit_solution(11803177568052185892)
XLA Ops:
  0.0 1.3 %fusion = (s32[1]{0:T(128)}, s32[1]{0:T(128)}) fusion(s32[8]{0:T(128)} %param.5, s32[]{:T(128)S(6)} %select_n.14, s32[]{:T(128)S(6)} %select_n.16), kind=kLoop, calls=%fused_computation.7 | loop fusion | bytes 24 | tf_op jit(solution)/shard_map/jit(dynamic_index_in_dim)/dynamic_slice | solution.py:120
  2.5 0.7 %select_reduce_fusion.inverse = s32[8]{0:T(128)S(1)} fusion(s32[8]{0:T(128)} %param.4), kind=kLoop, calls=%fused_computation.3 | loop fusion | flops 184 | bytes 64 | tf_op jit(solution)/shard_map/reduce_sum | solution.py:108
  3.3 1.2 %reshape.6 = bf16[512,2,256]{2,1,0:T(2,128)(2,1)S(1)} reshape(bf16[512,512]{1,0:T(8,128)(2,1)} %param.3) | data formatting | bytes 1048576 | tf_op jit(solution)/shard_map/reshape | solution.py:116
  4.4 1.1 %constant_dynamic-slice_fusion = (bf16[512,1,256]{2,1,0:T(2,128)(2,1)S(1)}, bf16[512,1,256]{2,1,0:T(2,128)(2,1)S(1)}) fusion(bf16[512,2,256]{2,1,0:T(2,128)(2,1)S(1)} %reshape.6, s32[]{:T(128)S(6)} %select_n.15, s32[]{:T(128)S(6)} %select_n.17), kind=kLoop, calls=%fused_computation.5 | loop fusion | bytes 1048584 | tf_op jit(solution)/shard_map/jit(dynamic_index_in_dim)/dynamic_slice | solution.py:121
  5.5 0.1 copy_bitcast_fusion
  5.6 0.1 pad_maximum_fusion.pieces
  5.7 52.1 %gather.1.refs_0_ = bf16[8,2,512,256]{3,2,1,0:T(8,128)(2,1)S(1)} custom-call(bf16[2,512,256]{2,1,0:T(8,128)(2,1)S(1)} %pad_maximum_fusion.pieces), custom_call_target="tpu_custom_call" | custom-call | tf_op jit(solution)/shard_map/gather/pallas_call | solution.py:124
  57.8 5.6 %pack.1 = f32[512,4096]{1,0:T(8,128)} custom-call(s32[8]{0:T(128)S(1)} %select_reduce_fusion.inverse, bf16[8,2,512,256]{3,2,1,0:T(8,128)(2,1)S(1)} %gather.1.refs_0_), custom_call_target="tpu_custom_call" | custom-call | tf_op jit(solution)/shard_map/pack/pallas_call | solution.py:142

commit v2 on v1

v2 whole, which is shorter than its diff:
```python
import functools

import jax
import jax.numpy as jnp
from jax import lax
from jax.experimental import pallas as pl
from jax.experimental.pallas import tpu as pltpu
from jax.sharding import PartitionSpec as P

MESH = pl.DeviceIdType.MESH
CHUNKS = 2


def ring_member(position, n):
    half = position // (n // 2)
    return 2 * position * (1 - half) + (2 * (n - 1 - position) + 1) * half


def ring_position(member, n):
    odd = member % 2
    return (member // 2) * (1 - odd) + (n - 1 - member // 2) * odd


def pick_kernel(head_map, source, picked):
    picked[0] = source[...]


def gather_kernel(n, tp, pieces, gathered, carried, x_send, x_recv, r_send, r_recv, d_send, d_recv, o_send, o_recv):
    rows = pieces.shape[1]
    me, k = lax.axis_index("grp"), lax.axis_index("tp")
    position = ring_position(me, n)
    ring = [ring_member((position + 1) % n, n), ring_member((position + n - 1) % n, n)]
    size = rows // (2 * CHUNKS)
    every = [(c, way) for c in range(CHUNKS) for way in range(2)]
    served = [(k + 2 * tp - tp // 2 - i) % tp for i in range(2)]

    barrier = pltpu.get_barrier_semaphore()
    for step in range(1, tp):
        pl.semaphore_signal(barrier, inc=1, device_id=(me, (k + step) % tp), device_id_type=MESH)
    for other in ring:
        pl.semaphore_signal(barrier, inc=1, device_id=(other, k), device_id_type=MESH)
    pl.semaphore_wait(barrier, tp + 1)

    def span(c, way):
        return pl.ds((way * CHUNKS + c) * size, size)

    def send(src, dst, send_sem, recv_sem, to):
        return pltpu.make_async_remote_copy(
            src_ref=src, dst_ref=dst, send_sem=send_sem, recv_sem=recv_sem,
            device_id=to, device_id_type=MESH,
        )

    def held(step, way):
        return ring_member((position + (n - step if way == 0 else step)) % n, n)

    def exchange(c, way):
        return send(pieces.at[0, span(c, way)], gathered.at[me, 0, span(c, way)],
                    x_send.at[way, c], x_recv.at[way, c], (me, served[0]))

    def own(c, way):
        return send(pieces.at[1, span(c, way)], gathered.at[me, 1, span(c, way)],
                    o_send.at[way, c], o_recv.at[way, c], (me, served[1]))

    def hop(step, c, way):
        chunk = gathered.at[held(step, way), 0, span(c, way)]
        return send(chunk, chunk, r_send.at[step, way, c], r_recv.at[step, way, c], (ring[way], k))

    def first(c, way):
        return send(pieces.at[1, span(c, way)], carried.at[me, span(c, way)],
                    r_send.at[0, way, CHUNKS + c], r_recv.at[0, way, CHUNKS + c], (ring[way], k))

    def carry(step, c, way):
        chunk = carried.at[held(step, way), span(c, way)]
        return send(chunk, chunk, r_send.at[step, way, CHUNKS + c], r_recv.at[step, way, CHUNKS + c],
                    (ring[way], k))

    def hand(step, c, way):
        owner = held(step, way)
        return send(carried.at[owner, span(c, way)], gathered.at[owner, 1, span(c, way)],
                    d_send.at[step - 1, way, c], d_recv.at[step - 1, way, c], (me, served[1]))

    for c, way in every:
        exchange(c, way).start()
    for c, way in every:
        first(c, way).start()
    for c, way in every:
        exchange(c, way).wait_recv()
        hop(0, c, way).start()
    for c, way in every:
        own(c, way).start()

    def forward(step, _):
        for c, way in every:
            carry(step - 1, c, way).wait_recv()
            carry(step, c, way).start()
            hand(step, c, way).start()
        for c, way in every:
            hop(step - 1, c, way).wait_recv()
            hop(step, c, way).start()
        return _

    lax.fori_loop(1, n - 1, forward, 0)
    for c, way in every:
        carry(n - 2, c, way).wait_recv()
        hand(n - 1, c, way).start()
    for c, way in every:
        own(c, way).wait()
        exchange(c, way).wait_send()

    def drain(step, _):
        for c, way in every:
            hop(step, c, way).wait_send()
            carry(step, c, way).wait_send()
            hand(step + 1, c, way).wait()
        return _

    lax.fori_loop(0, n - 2, drain, 0)
    for c, way in every:
        hop(n - 2, c, way).wait_recv()
    drain(n - 2, 0)


def pack_kernel(order, *refs):
    blocks, out = refs[:-1], refs[-1]
    slots, width = blocks[0].shape[1], blocks[0].shape[3] // 2
    for c in range(2):
        for i in range(slots):
            cut = [b[0, i, :, c * width:(c + 1) * width] for b in blocks]
            whole = cut[0] if len(cut) == 1 else jnp.concatenate(cut, axis=0)
            out[pl.ds((c * slots + i) * width, width), :] = whole.T.astype(jnp.float32)


def invert_order(span_order):
    block_count = span_order.shape[0]
    positions = jnp.arange(block_count, dtype=jnp.int32)
    matches = (span_order[:, None] == positions[None, :]).astype(jnp.int32)
    return jnp.sum(matches * positions[:, None], axis=0)


def local(n, tp, source_rows, span_order, head_map):
    rows = source_rows.shape[0]
    slots = head_map.shape[0] // tp
    columns = source_rows.shape[1] // slots

    def head(i, head_map):
        k = lax.axis_index("tp")
        served = lax.rem(k + 2 * tp - tp // 2 - i, tp)
        return 0, head_map[served * slots + i] - k * slots

    pieces = pl.pallas_call(
        pick_kernel,
        out_shape=jax.ShapeDtypeStruct((slots, rows, columns), source_rows.dtype),
        grid_spec=pltpu.PrefetchScalarGridSpec(
            num_scalar_prefetch=1,
            grid=(slots,),
            in_specs=[pl.BlockSpec((rows, columns), head)],
            out_specs=pl.BlockSpec((1, rows, columns), lambda i, head_map: (i, 0, 0)),
        ),
        compiler_params=pltpu.CompilerParams(vmem_limit_bytes=4 * 1024 * 1024),
        name="pick",
    )(head_map, source_rows)
    gathered = pl.pallas_call(
        functools.partial(gather_kernel, n, tp),
        out_shape=jax.ShapeDtypeStruct((n, slots, rows, columns), source_rows.dtype),
        in_specs=[pl.BlockSpec(memory_space=pl.ANY)],
        out_specs=pl.BlockSpec(memory_space=pl.ANY),
        scratch_shapes=[pltpu.VMEM((n, rows, columns), source_rows.dtype)]
        + [pltpu.SemaphoreType.DMA((2, CHUNKS))] * 2
        + [pltpu.SemaphoreType.DMA((n - 1, 2, 2 * CHUNKS))] * 2
        + [pltpu.SemaphoreType.DMA((n - 1, 2, CHUNKS))] * 2
        + [pltpu.SemaphoreType.DMA((2, CHUNKS))] * 2,
        compiler_params=pltpu.CompilerParams(
            collective_id=0, has_side_effects=True, vmem_limit_bytes=8 * 1024 * 1024
        ),
        name="gather",
    )(pieces)
    together = max(1, 128 // rows)
    if together == 1:
        order = span_order
        reads, writes = [lambda p, order: (p, 0, 0, 0)], lambda p, order: (0, order[p])
    else:
        order = invert_order(span_order)
        reads = [
            functools.partial(lambda j, p, order: (order[p * together + j], 0, 0, 0), j)
            for j in range(together)
        ]
        writes = lambda p, order: (0, p)
    packed = pl.pallas_call(
        pack_kernel,
        out_shape=jax.ShapeDtypeStruct((slots * columns, n * rows), jnp.float32),
        grid_spec=pltpu.PrefetchScalarGridSpec(
            num_scalar_prefetch=1,
            grid=(n // together,),
            in_specs=[pl.BlockSpec((1, slots, rows, columns), read) for read in reads],
            out_specs=pl.BlockSpec((slots * columns, together * rows), writes),
        ),
        compiler_params=pltpu.CompilerParams(vmem_limit_bytes=16 * 1024 * 1024),
        name="pack",
    )(order, *[gathered] * together)
    return packed


def solution(mesh):
    n, tp = mesh.shape["grp"], mesh.shape["tp"]
    placed = (P("grp", "tp"), P(), P())
    return jax.shard_map(
        functools.partial(local, n, tp), mesh=mesh, in_specs=placed,
        out_specs=P("tp", None), check_vma=False,
    )
```

time: 63.6 us -> 58.4 us (0.918)
  Pallas kernels: 57.7 us -> 55.8 us
  local copies, waits for them, and re-layouts: 3.66 us -> 2.35 us
  between operations: 1.26 us -> 0.03 us
  other arithmetic: 0.79 us -> 0 us
    pallas_call x1, Pallas kernels: 52.1 us -> 49.5 us  [local(): pl.pallas_call(functools.partial(gather_kernel, n, tp), out_shape=jax.Sha...]
    dynamic_slice x2 -> x0, local copies, waits for them, and re-layouts: 2.4 us -> none  [the longest x1 1.31 us: local(): lax.dynamic_index_in_dim(head_map, served * slots + i, keepdims=False)]
    unnamed x0 -> x6, local copies, waits for them, and re-layouts: none -> 2.35 us
    reshape x1 -> x0, local copies, waits for them, and re-layouts: 1.16 us -> none  [local(): heads = source_rows.reshape(rows, slots, columns)]
    pallas_call x0 -> x1, Pallas kernels: none -> 0.76 us  [local(): pl.pallas_call(pick_kernel, out_shape=jax.ShapeDtypeStruct((slots, rows,...]
    reduce_sum x1 -> x0, other arithmetic: 0.74 us -> none  [invert_order(): return jnp.sum(matches * positions[:, None], axis=0)]
where the time goes in v2:
time: 58.4 us; the launch traced here: 58.2 us
  Pallas kernels  55.8 us (96%)
  local copies, waits for them, and re-layouts  2.35 us (4%)
    pallas_call x1, Pallas kernels, local(): pl.pallas_call(functools.partial(gather_kernel, n, tp), out_shape=jax.Sha...  49.5 us
    pallas_call x1, Pallas kernels, local(): pl.pallas_call(pack_kernel, out_shape=jax.ShapeDtypeStruct((slots * colum...  5.54 us
    unnamed x6, local copies, waits for them, and re-layouts  2.35 us

profile of v2, /device:TPU:0, one launch (start us, length us, event | category | flops | bytes accessed | tf_op | source)
XLA Modules:
  0.0 58.2 jit_solution(1974330071107241015)
XLA Ops:
  0.0 0.0 copy-start
  0.0 1.0 %copy-done = bf16[512,512]{1,0:T(8,128)(2,1)S(1)} copy-done((bf16[512,512]{1,0:T(8,128)(2,1)S(1)}, bf16[512,512]{1,0:T(8,128)(2,1)}, u32[]{:S(2)}) %copy-start) | copy-done | bytes 524312
  1.0 0.0 copy-start.1
  1.0 0.7 %copy-done.1 = s32[8]{0:T(128)S(1)} copy-done((s32[8]{0:T(128)S(1)}, s32[8]{0:T(128)}, u32[]{:S(2)}) %copy-start.1) | copy-done | bytes 56
  1.7 0.8 %pick.1.pieces = bf16[2,512,256]{2,1,0:T(8,128)(2,1)S(1)} custom-call(s32[8]{0:T(128)S(1)} %copy-done.1, bf16[512,512]{1,0:T(8,128)(2,1)S(1)} %copy-done), custom_call_target="tpu_custom_call" | custom-call | tf_op jit(solution)/shard_map/pick/pallas_call | solution.py:150
  2.5 49.5 %gather.1.refs_0_ = bf16[8,2,512,256]{3,2,1,0:T(8,128)(2,1)S(1)} custom-call(bf16[2,512,256]{2,1,0:T(8,128)(2,1)S(1)} %pick.1.pieces), custom_call_target="tpu_custom_call" | custom-call | tf_op jit(solution)/shard_map/gather/pallas_call | solution.py:162
  52.0 0.0 copy-start.2
  52.0 0.6 %copy-done.2 = s32[8]{0:T(128)S(1)} copy-done((s32[8]{0:T(128)S(1)}, s32[8]{0:T(128)}, u32[]{:S(2)}) %copy-start.2) | copy-done | bytes 56
  52.7 5.5 %pack.1 = f32[512,4096]{1,0:T(8,128)} custom-call(s32[8]{0:T(128)S(1)} %copy-done.2, bf16[8,2,512,256]{3,2,1,0:T(8,128)(2,1)S(1)} %gather.1.refs_0_), custom_call_target="tpu_custom_call" | custom-call | tf_op jit(solution)/shard_map/pack/pallas_call | solution.py:188
Async XLA Ops:
  0.0 1.0 %copy-start = (bf16[512,512]{1,0:T(8,128)(2,1)S(1)}, bf16[512,512]{1,0:T(8,128)(2,1)}, u32[]{:S(2)}) copy-start(bf16[512,512]{1,0:T(8,128)(2,1)} %source.1) | copy-start | bytes 1572868
  1.0 0.7 %copy-start.1 = (s32[8]{0:T(128)S(1)}, s32[8]{0:T(128)}, u32[]{:S(2)}) copy-start(s32[8]{0:T(128)} %head_map.1) | copy-start | bytes 100
  52.0 0.7 %copy-start.2 = (s32[8]{0:T(128)S(1)}, s32[8]{0:T(128)}, u32[]{:S(2)}) copy-start(s32[8]{0:T(128)} %order.1) | copy-start | bytes 100

commit v3 on v2

--- a/solution.py
+++ b/solution.py
@@ -21,11 +21,13 @@
     return (member // 2) * (1 - odd) + (n - 1 - member // 2) * odd
 
 
-def pick_kernel(head_map, source, picked):
-    picked[0] = source[...]
-
-
-def gather_kernel(n, tp, pieces, gathered, carried, x_send, x_recv, r_send, r_recv, d_send, d_recv, o_send, o_recv):
+def gather_kernel(n, tp, slots, source, head_map, gathered, block, heads, pieces, carried, load, x_send, x_recv, r_send, r_recv, d_send, d_recv, o_send, o_recv):
+    loads = [
+        pltpu.make_async_copy(head_map, heads, load.at[0]),
+        pltpu.make_async_copy(source, block, load.at[1]),
+    ]
+    for copy in loads:
+        copy.start()
     rows = pieces.shape[1]
     me, k = lax.axis_index("grp"), lax.axis_index("tp")
     position = ring_position(me, n)
@@ -39,6 +41,15 @@
         pl.semaphore_signal(barrier, inc=1, device_id=(me, (k + step) % tp), device_id_type=MESH)
     for other in ring:
         pl.semaphore_signal(barrier, inc=1, device_id=(other, k), device_id_type=MESH)
+    for copy in loads:
+        copy.wait()
+    columns = pieces.shape[2]
+    for i in range(slots):
+        head = heads[served[i] * slots + i] - k * slots
+        chosen = block[:, :columns]
+        for j in range(1, slots):
+            chosen = jnp.where(head == j, block[:, j * columns:(j + 1) * columns], chosen)
+        pieces[i] = chosen
     pl.semaphore_wait(barrier, tp + 1)
 
     def span(c, way):
@@ -83,26 +94,37 @@
         exchange(c, way).start()
     for c, way in every:
         first(c, way).start()
-    for c, way in every:
-        exchange(c, way).wait_recv()
-        hop(0, c, way).start()
+    both = range(2)
+    for c in range(CHUNKS):
+        for way in both:
+            exchange(c, way).wait_recv()
+            hop(0, c, way).start()
+        for way in both:
+            carry(0, c, way).wait_recv()
+            carry(1, c, way).start()
     for c, way in every:
         own(c, way).start()
+        hand(1, c, way).start()
 
     def forward(step, _):
-        for c, way in every:
-            carry(step - 1, c, way).wait_recv()
-            carry(step, c, way).start()
-            hand(step, c, way).start()
-        for c, way in every:
-            hop(step - 1, c, way).wait_recv()
-            hop(step, c, way).start()
+        for c in range(CHUNKS):
+            for way in both:
+                hop(step - 1, c, way).wait_recv()
+                hop(step, c, way).start()
+            for way in both:
+                carry(step, c, way).wait_recv()
+                carry(step + 1, c, way).start()
+                hand(step + 1, c, way).start()
         return _
 
-    lax.fori_loop(1, n - 1, forward, 0)
-    for c, way in every:
-        carry(n - 2, c, way).wait_recv()
-        hand(n - 1, c, way).start()
+    lax.fori_loop(1, n - 2, forward, 0)
+    for c in range(CHUNKS):
+        for way in both:
+            hop(n - 3, c, way).wait_recv()
+            hop(n - 2, c, way).start()
+        for way in both:
+            carry(n - 2, c, way).wait_recv()
+            hand(n - 1, c, way).start()
     for c, way in every:
         own(c, way).wait()
         exchange(c, way).wait_send()
@@ -118,6 +140,26 @@
     for c, way in every:
         hop(n - 2, c, way).wait_recv()
     drain(n - 2, 0)
+
+
+def place_kernel(order, gathered, out, order_here, ready, load, sems):
+    n, slots, rows, columns = gathered.shape
+    width = columns // 2
+    fetch = pltpu.make_async_copy(order, order_here, load)
+    fetch.start()
+    copies = []
+    for p in range(n):
+        for c in range(2):
+            for i in range(slots):
+                cut = gathered[p, i, :, c * width:(c + 1) * width]
+                ready[p, pl.ds((c * slots + i) * width, width), :] = cut.T.astype(jnp.float32)
+        if p == 0:
+            fetch.wait()
+        start = pl.multiple_of(order_here[p] * rows, 128)
+        copies.append(pltpu.make_async_copy(ready.at[p], out.at[:, pl.ds(start, rows)], sems.at[p]))
+        copies[-1].start()
+    for copy in copies:
+        copy.wait()
 
 
 def pack_kernel(order, *refs):
@@ -141,50 +183,50 @@
     rows = source_rows.shape[0]
     slots = head_map.shape[0] // tp
     columns = source_rows.shape[1] // slots
-
-    def head(i, head_map):
-        k = lax.axis_index("tp")
-        served = lax.rem(k + 2 * tp - tp // 2 - i, tp)
-        return 0, head_map[served * slots + i] - k * slots
-
-    pieces = pl.pallas_call(
-        pick_kernel,
-        out_shape=jax.ShapeDtypeStruct((slots, rows, columns), source_rows.dtype),
-        grid_spec=pltpu.PrefetchScalarGridSpec(
-            num_scalar_prefetch=1,
-            grid=(slots,),
-            in_specs=[pl.BlockSpec((rows, columns), head)],
-            out_specs=pl.BlockSpec((1, rows, columns), lambda i, head_map: (i, 0, 0)),
-        ),
-        compiler_params=pltpu.CompilerParams(vmem_limit_bytes=4 * 1024 * 1024),
-        name="pick",
-    )(head_map, source_rows)
+    dtype = source_rows.dtype
+    sems = pltpu.SemaphoreType.DMA
     gathered = pl.pallas_call(
-        functools.partial(gather_kernel, n, tp),
-        out_shape=jax.ShapeDtypeStruct((n, slots, rows, columns), source_rows.dtype),
-        in_specs=[pl.BlockSpec(memory_space=pl.ANY)],
+        functools.partial(gather_kernel, n, tp, slots),
+        out_shape=jax.ShapeDtypeStruct((n, slots, rows, columns), dtype),
+        in_specs=[pl.BlockSpec(memory_space=pltpu.HBM)] * 2,
         out_specs=pl.BlockSpec(memory_space=pl.ANY),
-        scratch_shapes=[pltpu.VMEM((n, rows, columns), source_rows.dtype)]
-        + [pltpu.SemaphoreType.DMA((2, CHUNKS))] * 2
-        + [pltpu.SemaphoreType.DMA((n - 1, 2, 2 * CHUNKS))] * 2
-        + [pltpu.SemaphoreType.DMA((n - 1, 2, CHUNKS))] * 2
-        + [pltpu.SemaphoreType.DMA((2, CHUNKS))] * 2,
+        scratch_shapes=[
+            pltpu.VMEM(source_rows.shape, dtype),
+            pltpu.SMEM(head_map.shape, head_map.dtype),
+            pltpu.VMEM((slots, rows, columns), dtype),
+            pltpu.VMEM((n, rows, columns), dtype),
+            sems((2,)),
+        ]
+        + [sems((2, CHUNKS))] * 2
+        + [sems((n - 1, 2, 2 * CHUNKS))] * 2
+        + [sems((n - 1, 2, CHUNKS))] * 2
+        + [sems((2, CHUNKS))] * 2,
         compiler_params=pltpu.CompilerParams(
             collective_id=0, has_side_effects=True, vmem_limit_bytes=8 * 1024 * 1024
         ),
         name="gather",
-    )(pieces)
+    )(*[pltpu.with_memory_space_constraint(a, pltpu.HBM) for a in (source_rows, head_map)])
+    if rows % 128 == 0:
+        return pl.pallas_call(
+            place_kernel,
+            out_shape=jax.ShapeDtypeStruct((slots * columns, n * rows), jnp.float32),
+            in_specs=[pl.BlockSpec(memory_space=pltpu.HBM), pl.BlockSpec(memory_space=pltpu.VMEM)],
+            out_specs=pl.BlockSpec(memory_space=pltpu.HBM),
+            scratch_shapes=[
+                pltpu.SMEM(span_order.shape, span_order.dtype),
+                pltpu.VMEM((n, slots * columns, rows), jnp.float32),
+                pltpu.SemaphoreType.DMA,
+                sems((n,)),
+            ],
+            compiler_params=pltpu.CompilerParams(vmem_limit_bytes=24 * 1024 * 1024),
+            name="place",
+        )(pltpu.with_memory_space_constraint(span_order, pltpu.HBM), gathered)
     together = max(1, 128 // rows)
-    if together == 1:
-        order = span_order
-        reads, writes = [lambda p, order: (p, 0, 0, 0)], lambda p, order: (0, order[p])
-    else:
-        order = invert_order(span_order)
-        reads = [
-            functools.partial(lambda j, p, order: (order[p * together + j], 0, 0, 0), j)
-            for j in range(together)
-        ]
-        writes = lambda p, order: (0, p)
+    inverse = invert_order(span_order)
+    reads = [
+        functools.partial(lambda j, b, order: (order[b * together + j], 0, 0, 0), j)
+        for j in range(together)
+    ]
     packed = pl.pallas_call(
         pack_kernel,
         out_shape=jax.ShapeDtypeStruct((slots * columns, n * rows), jnp.float32),
@@ -192,11 +234,11 @@
             num_scalar_prefetch=1,
             grid=(n // together,),
             in_specs=[pl.BlockSpec((1, slots, rows, columns), read) for read in reads],
-            out_specs=pl.BlockSpec((slots * columns, together * rows), writes),
+            out_specs=pl.BlockSpec((slots * columns, together * rows), lambda b, order: (0, b)),
         ),
         compiler_params=pltpu.CompilerParams(vmem_limit_bytes=16 * 1024 * 1024),
         name="pack",
-    )(order, *[gathered] * together)
+    )(inverse, *[gathered] * together)
     return packed
 
 

time: 58.4 us -> 54 us (0.925)
  local copies, waits for them, and re-layouts: 2.35 us -> 0 us
  Pallas kernels: 55.8 us -> 53.8 us
    unnamed x6 -> x0, local copies, waits for them, and re-layouts: 2.35 us -> none
    pallas_call x3 -> x2, Pallas kernels: 55.8 us -> 53.8 us  [the longest x1 49.8 us: local(): pl.pallas_call(functools.partial(gather_kernel, n, tp, slots), out_shape=...]
where the time goes in v3:
time: 54 us; the launch traced here: 53.9 us
  Pallas kernels  53.8 us (100%)
    pallas_call x1, Pallas kernels, local(): pl.pallas_call(functools.partial(gather_kernel, n, tp, slots), out_shape=...  49.8 us
    pallas_call x1, Pallas kernels, local(): pl.pallas_call(place_kernel, out_shape=jax.ShapeDtypeStruct((slots * colu...  4.05 us

profile of v3, /device:TPU:0, one launch (start us, length us, event | category | flops | bytes accessed | tf_op | source)
XLA Modules:
  0.0 53.9 jit_solution(5325162787404777652)
XLA Ops:
  0.0 49.8 %gather.1.gathered = bf16[8,2,512,256]{3,2,1,0:T(8,128)(2,1)S(1)} custom-call(bf16[512,512]{1,0:T(8,128)(2,1)} %source.1, s32[8]{0:T(128)} %head_map.1), custom_call_target="tpu_custom_call" | custom-call | tf_op jit(solution)/shard_map/gather/pallas_call | solution.py:188
  49.8 4.0 %place.1 = f32[512,4096]{1,0:T(8,128)} custom-call(s32[8]{0:T(128)} %order.1, bf16[8,2,512,256]{3,2,1,0:T(8,128)(2,1)S(1)} %gather.1.gathered), custom_call_target="tpu_custom_call" | custom-call | tf_op jit(solution)/shard_map/place/pallas_call | solution.py:210

commit v4 on v3

--- a/solution.py
+++ b/solution.py
@@ -148,16 +148,21 @@
     fetch = pltpu.make_async_copy(order, order_here, load)
     fetch.start()
     copies = []
+    half = slots * width
     for p in range(n):
         for c in range(2):
             for i in range(slots):
                 cut = gathered[p, i, :, c * width:(c + 1) * width]
                 ready[p, pl.ds((c * slots + i) * width, width), :] = cut.T.astype(jnp.float32)
-        if p == 0:
-            fetch.wait()
-        start = pl.multiple_of(order_here[p] * rows, 128)
-        copies.append(pltpu.make_async_copy(ready.at[p], out.at[:, pl.ds(start, rows)], sems.at[p]))
-        copies[-1].start()
+            if p == 0 and c == 0:
+                fetch.wait()
+            start = pl.multiple_of(order_here[p] * rows, 128)
+            copies.append(pltpu.make_async_copy(
+                ready.at[p, pl.ds(c * half, half)],
+                out.at[pl.ds(c * half, half), pl.ds(start, rows)],
+                sems.at[p, c],
+            ))
+            copies[-1].start()
     for copy in copies:
         copy.wait()
 
@@ -216,7 +221,7 @@
                 pltpu.SMEM(span_order.shape, span_order.dtype),
                 pltpu.VMEM((n, slots * columns, rows), jnp.float32),
                 pltpu.SemaphoreType.DMA,
-                sems((n,)),
+                sems((n, 2)),
             ],
             compiler_params=pltpu.CompilerParams(vmem_limit_bytes=24 * 1024 * 1024),
             name="place",

time: 54 us -> 54.1 us (level)
  no operation moved by 1% of the time
where the time goes in v4:
time: 54.1 us; the launch traced here: 53.9 us
  Pallas kernels  53.9 us (100%)
    pallas_call x1, Pallas kernels, local(): pl.pallas_call(functools.partial(gather_kernel, n, tp, slots), out_shape=...  49.8 us
    pallas_call x1, Pallas kernels, local(): pl.pallas_call(place_kernel, out_shape=jax.ShapeDtypeStruct((slots * colu...  4.1 us

profile of v4, /device:TPU:0, one launch (start us, length us, event | category | flops | bytes accessed | tf_op | source)
XLA Modules:
  0.0 53.9 jit_solution(4491855666220023601)
XLA Ops:
  0.0 49.8 %gather.1.gathered = bf16[8,2,512,256]{3,2,1,0:T(8,128)(2,1)S(1)} custom-call(bf16[512,512]{1,0:T(8,128)(2,1)} %source.1, s32[8]{0:T(128)} %head_map.1), custom_call_target="tpu_custom_call" | custom-call | tf_op jit(solution)/shard_map/gather/pallas_call | solution.py:193
  49.8 4.1 %place.1 = f32[512,4096]{1,0:T(8,128)} custom-call(s32[8]{0:T(128)} %order.1, bf16[8,2,512,256]{3,2,1,0:T(8,128)(2,1)S(1)} %gather.1.gathered), custom_call_target="tpu_custom_call" | custom-call | tf_op jit(solution)/shard_map/place/pallas_call | solution.py:215
